TPU v7x, 32 devices: a whole 2x2x4 slice. The times are simulated.
32 devices in a mesh: layer: 8 (over y, x, core), latent: 4 (over z).
Axes of the slice: x: 2, y: 2, z: 4, core: 2. Of those that a mesh axis runs over, the one named last changes fastest.
Arguments:
- decoder: bfloat16 [65536, 4, 2304], P(('layer', 'latent')), may hold values from -0.375 to 0.375
- code_index: int32 [4, 128, 64], replicated, may hold values from 0 to 16383, all different within a row
- code_value: bfloat16 [4, 128, 64], replicated, may hold values from 0.19921875 to 4
- bias: float32 [4, 2304], replicated, may hold values from -3 to 3
- target: bfloat16 [4, 128, 2304], replicated, may hold values from -6 to 6
Outputs:
- layer_error: float32 [4], replicated
- grad_decoder: bfloat16 [65536, 4, 2304], P(('layer', 'latent'))
- code_grad: float32 [4, 128, 64], replicated
Inputs may be any that keep to these rules, and one draw needn't show every extreme that they name: `code_index`: the 64 indices of one token in one layer are distinct.
All inputs are finite; a program needn't handle non-finite values.
Results may differ from a plain program's by a relative error of at most 0.0048.
Values may be sent and summed in bfloat16 or wider, within the bound.
No kernel may reach another device: no remote copies, remote signals or barrier semaphores. Data moves between devices by JAX's collectives and lax.ppermute only.
A program may use at most 192 MiB of HBM per device.

v0:
```python
import jax
import jax.numpy as jnp
from jax import lax
from jax.sharding import PartitionSpec as P

D = 2304
LAYERS = 4
TOPK = 64
TOKENS = 128


def build_codes(index_rows, value_rows, offset, slab_width):
    columns = offset + lax.iota(jnp.int32, slab_width)
    matches = index_rows[:, :, None] == columns[None, None, :]
    dense = jnp.sum(jnp.where(matches, value_rows[:, :, None].astype(jnp.float32), 0.0), axis=1)
    return (matches, dense.astype(jnp.bfloat16))


def contract_rows(left, right):
    return lax.dot_general(
        left, right, (((0,), (0,)), ((), ())), preferred_element_type=jnp.float32
    )


def contract_cols(left, right):
    return lax.dot_general(
        left, right, (((1,), (1,)), ((), ())), preferred_element_type=jnp.float32
    )


def on_device(decoder, code_index, code_value, bias, target):
    layer_count = lax.axis_size("layer")
    latent_count = lax.axis_size("latent")
    group_size = layer_count // LAYERS
    slab_width = decoder.shape[0]
    layer_pos = lax.axis_index("layer")
    source = layer_pos // group_size
    offset = (layer_pos % group_size * latent_count + lax.axis_index("latent")) * slab_width
    matches, dense_codes = build_codes(
        lax.dynamic_index_in_dim(code_index, source, 0, keepdims=False),
        lax.dynamic_index_in_dim(code_value, source, 0, keepdims=False),
        offset,
        slab_width,
    )

    def forward_step(target_layer, totals):
        weight_slab = lax.dynamic_index_in_dim(decoder, target_layer, 1, keepdims=False)
        product = jnp.dot(dense_codes, weight_slab, preferred_element_type=jnp.float32)
        return lax.dynamic_update_index_in_dim(totals, product, target_layer, 0)

    partials = jnp.zeros((LAYERS, TOKENS, D), jnp.float32)
    stop_at = LAYERS
    partials = lax.fori_loop(source, stop_at, forward_step, partials)
    recon_sum = lax.psum(partials, ("layer", "latent"))
    residual = recon_sum + bias[:, None, :] - target.astype(jnp.float32)
    layer_error = jnp.mean(residual * residual, axis=(1, 2))
    error_b = residual.astype(jnp.bfloat16)

    def backward_step(target_layer, state_pair):
        grads, code_sums = state_pair
        weight_slab = lax.dynamic_index_in_dim(decoder, target_layer, 1, keepdims=False)
        target_error = lax.dynamic_index_in_dim(error_b, target_layer, 0, keepdims=False)
        grad_block = contract_rows(dense_codes, target_error).astype(jnp.bfloat16)
        grads = lax.dynamic_update_index_in_dim(grads, grad_block, target_layer, 1)
        return (grads, code_sums + contract_cols(target_error, weight_slab))

    start_pair = (
        jnp.zeros(decoder.shape, jnp.bfloat16),
        jnp.zeros((TOKENS, slab_width), jnp.float32),
    )
    grads, code_sums = lax.fori_loop(source, stop_at, backward_step, start_pair)
    picked = jnp.sum(jnp.where(matches, code_sums[:, None, :], 0.0), axis=2)
    code_parts = lax.dynamic_update_index_in_dim(
        jnp.zeros((LAYERS, TOKENS, TOPK), jnp.float32), picked, source, 0
    )
    code_grad = lax.psum(code_parts, ("layer", "latent"))
    return (layer_error, grads, code_grad)


def solution(mesh):
    placed = (P(("layer", "latent"), None, None), P(), P(), P(), P())
    return jax.shard_map(
        on_device,
        mesh=mesh,
        in_specs=placed,
        out_specs=(P(), P(("layer", "latent"), None, None), P()),
        check_vma=False,
    )
```

profile of v0, /device:TPU:0, one launch (start us, length us, event | category | flops | bytes accessed | tf_op | source)
XLA Modules:
  0.0 428.5 jit_solution(2103701920801345203)
XLA Ops:
  7.2 0.0 copy-start
  7.2 0.0 all-reduce.3.cloned.1.call-start
  7.2 25.9 %copy.19 = bf16[2048,4,2304]{2,0,1:T(8,128)(2,1)} copy(bf16[2048,4,2304]{2,1,0:T(4,128)(2,1)} %param.9) | data formatting | bytes 75497472 | tf_op jit(solution)/shard_map/while | solution.py:53
  33.1 0.7 bitcast_convert_fusion
  33.8 0.1 copy.18
  34.0 0.0 copy-done
  34.0 0.1 copy.17
  34.1 9.8 %fusion.21 = bf16[128,2048]{1,0:T(8,128)(2,1)S(1)} fusion(f32[128,64]{1,0:T(8,128)S(1)} %copy.18, s32[2048]{0:T(1024)S(1)} %iota_add_fusion, s32[128,64]{1,0:T(8,128)S(1)} %copy.17), kind=kLoop, calls=%fused_computation.21 | loop fusion | flops 50069504 | bytes 598016 | tf_op jit(solution)/shard_map/reduce_sum | solution.py:15
  43.9 2.6 broadcast_in_dim.51.clone
  46.5 0.0 copy-start.4
  46.5 26.9 %while.22 = (s32[]{:T(128)}, f32[4,128,2304]{2,1,0:T(8,128)}, bf16[2048,4,2304]{2,0,1:T(8,128)(2,1)}, bf16[128,2048]{1,0:T(8,128)(2,1)S(1)}, s32[]{:T(128)}, /*index=5*/s32[]{:T(128)}, s32[]{:T(128)}) while((s32[]{:T(128)}, f32[4,128,2304]{2,1,0:T(8,128)}, bf16[2048,4,2304]{2,0,1:T(8,128)(2,1)}, bf16[128,2048]{1,0:T(8,128)(2,1)S(1)}, ...), condition=%wide.region_2.3_spmd, body=%wide.region_1.2_spmd.sunk | while | flops 1207959552 | bytes 15859839 | solution.py:53
  46.5 5.2 %fusion.37 = f32[1,128,2304]{1,2,0:T(8,128)S(1)} fusion(bf16[128,2048]{1,0:T(8,128)(2,1)S(1)} %get-tuple-element.191, bf16[2048,4,2304]{2,0,1:T(8,128)(2,1)} %get-tuple-element.190, s32[]{:T(128)S(6)} %select_n.53), kind=kOutput, calls=%fused_computation.3.clone.1 | convolution fusion | flops 1207959552 | bytes 11141124 | tf_op jit(solution)/shard_map/while/body/dot_general | solution.py:48
  51.7 0.4 copy.30
  52.1 1.1 constant_dynamic-update-slice_fusion.3
  53.2 5.2 %fusion.37 = f32[1,128,2304]{1,2,0:T(8,128)S(1)} fusion(bf16[128,2048]{1,0:T(8,128)(2,1)S(1)} %get-tuple-element.191, bf16[2048,4,2304]{2,0,1:T(8,128)(2,1)} %get-tuple-element.190, s32[]{:T(128)S(6)} %select_n.53), kind=kOutput, calls=%fused_computation.3.clone.1 | convolution fusion | flops 1207959552 | bytes 11141124 | tf_op jit(solution)/shard_map/while/body/dot_general | solution.py:48
  58.4 0.4 copy.30
  58.8 1.1 constant_dynamic-update-slice_fusion.3
  59.9 5.2 %fusion.37 = f32[1,128,2304]{1,2,0:T(8,128)S(1)} fusion(bf16[128,2048]{1,0:T(8,128)(2,1)S(1)} %get-tuple-element.191, bf16[2048,4,2304]{2,0,1:T(8,128)(2,1)} %get-tuple-element.190, s32[]{:T(128)S(6)} %select_n.53), kind=kOutput, calls=%fused_computation.3.clone.1 | convolution fusion | flops 1207959552 | bytes 11141124 | tf_op jit(solution)/shard_map/while/body/dot_general | solution.py:48
  65.1 0.4 copy.30
  65.5 1.1 constant_dynamic-update-slice_fusion.3
  66.6 5.2 %fusion.37 = f32[1,128,2304]{1,2,0:T(8,128)S(1)} fusion(bf16[128,2048]{1,0:T(8,128)(2,1)S(1)} %get-tuple-element.191, bf16[2048,4,2304]{2,0,1:T(8,128)(2,1)} %get-tuple-element.190, s32[]{:T(128)S(6)} %select_n.53), kind=kOutput, calls=%fused_computation.3.clone.1 | convolution fusion | flops 1207959552 | bytes 11141124 | tf_op jit(solution)/shard_map/while/body/dot_general | solution.py:48
  71.8 0.4 copy.30
  72.2 1.2 constant_dynamic-update-slice_fusion.3
  73.4 0.0 copy-start.2
  73.4 0.0 all-reduce.3.cloned.1.call-update
  73.4 0.0 all-reduce.5.cloned.1.call-start
  73.5 145.7 %all-reduce.3.cloned.1.call-done = f32[4,128,2304]{2,1,0:T(8,128)} async-done(((f32[4,128,2304]{2,1,0:T(8,128)}), f32[4,128,2304]{2,1,0:T(8,128)}) %all-reduce.3.cloned.1.call-update) | async-done | bytes 4718608 | tf_op jit(solution)/shard_map/psum | solution.py:54
  219.2 0.0 copy-done.4
  219.2 4.1 fusion.23
  223.3 0.0 copy-done.2
  223.3 12.5 %broadcast_in_dim.54 = bf16[2048,4,2304]{0,2,1:T(8,128)(2,1)} broadcast(bf16[]{:T(256)} %constant.88.clone.1), dimensions={} | broadcast | bytes 37748736 | tf_op jit(solution)/shard_map/broadcast_in_dim | solution.py:68
  235.8 0.1 broadcast_in_dim.55
  235.9 52.3 %while.23 = (s32[]{:T(128)}, bf16[2048,4,2304]{0,2,1:T(8,128)(2,1)}, f32[128,2048]{1,0:T(8,128)S(1)}, bf16[4,128,2304]{2,1,0:T(8,128)(2,1)S(1)}, bf16[128,2048]{...) while((s32[]{:T(128)}, bf16[2048,4,2304]{0,2,1:T(8,128)(2,1)}, ...), condition=%wide.region_6.7_spmd, body=%wide.region_5.6_spmd.sunk | while | flops 2420899840 | bytes 22677640 | solution.py:71
  236.0 6.1 %fusion.42 = bf16[2048,4,2304]{0,2,1:T(8,128)(2,1)} fusion(bf16[2048,4,2304]{0,2,1:T(8,128)(2,1)} %get-tuple-element.205, s32[]{:T(128)S(6)} %select_n.54, bf16[128,2048]{1,0:T(8,128)(2,1)} %get-tuple-element.217, bf16[4,128,2304]{2,1,0:T(8,128)(2,1)S(1)} %get-tuple-element.216), kind=kOutput, calls=%fused_computation.8.clone.1 | convolution fusion | flops 1212678144 | bytes 10552320 | tf_op jit(solution)/shard_map/while/body/dot_general | solution.py:20
  242.1 6.9 %fusion.43 = f32[128,2048]{1,0:T(8,128)S(1)} fusion(f32[128,2048]{1,0:T(8,128)S(1)} %get-tuple-element.206, bf16[2048,4,2304]{2,0,1:T(8,128)(2,1)} %get-tuple-element.218, s32[]{:T(128)S(6)} %select_n.54, bf16[4,128,2304]{2,1,0:T(8,128)(2,1)S(1)} %get-tuple-element.216), kind=kOutput, calls=%fused_computation.12.clone.1 | convolution fusion | flops 1208221696 | bytes 12125184 | tf_op jit(solution)/shard_map/while/body/dot_general | solution.py:26
  249.0 6.1 %fusion.42 = bf16[2048,4,2304]{0,2,1:T(8,128)(2,1)} fusion(bf16[2048,4,2304]{0,2,1:T(8,128)(2,1)} %get-tuple-element.205, s32[]{:T(128)S(6)} %select_n.54, bf16[128,2048]{1,0:T(8,128)(2,1)} %get-tuple-element.217, bf16[4,128,2304]{2,1,0:T(8,128)(2,1)S(1)} %get-tuple-element.216), kind=kOutput, calls=%fused_computation.8.clone.1 | convolution fusion | flops 1212678144 | bytes 10552320 | tf_op jit(solution)/shard_map/while/body/dot_general | solution.py:20
  255.1 6.9 %fusion.43 = f32[128,2048]{1,0:T(8,128)S(1)} fusion(f32[128,2048]{1,0:T(8,128)S(1)} %get-tuple-element.206, bf16[2048,4,2304]{2,0,1:T(8,128)(2,1)} %get-tuple-element.218, s32[]{:T(128)S(6)} %select_n.54, bf16[4,128,2304]{2,1,0:T(8,128)(2,1)S(1)} %get-tuple-element.216), kind=kOutput, calls=%fused_computation.12.clone.1 | convolution fusion | flops 1208221696 | bytes 12125184 | tf_op jit(solution)/shard_map/while/body/dot_general | solution.py:26
  262.1 6.2 %fusion.42 = bf16[2048,4,2304]{0,2,1:T(8,128)(2,1)} fusion(bf16[2048,4,2304]{0,2,1:T(8,128)(2,1)} %get-tuple-element.205, s32[]{:T(128)S(6)} %select_n.54, bf16[128,2048]{1,0:T(8,128)(2,1)} %get-tuple-element.217, bf16[4,128,2304]{2,1,0:T(8,128)(2,1)S(1)} %get-tuple-element.216), kind=kOutput, calls=%fused_computation.8.clone.1 | convolution fusion | flops 1212678144 | bytes 10552320 | tf_op jit(solution)/shard_map/while/body/dot_general | solution.py:20
  268.3 6.9 %fusion.43 = f32[128,2048]{1,0:T(8,128)S(1)} fusion(f32[128,2048]{1,0:T(8,128)S(1)} %get-tuple-element.206, bf16[2048,4,2304]{2,0,1:T(8,128)(2,1)} %get-tuple-element.218, s32[]{:T(128)S(6)} %select_n.54, bf16[4,128,2304]{2,1,0:T(8,128)(2,1)S(1)} %get-tuple-element.216), kind=kOutput, calls=%fused_computation.12.clone.1 | convolution fusion | flops 1208221696 | bytes 12125184 | tf_op jit(solution)/shard_map/while/body/dot_general | solution.py:26
  275.2 6.1 %fusion.42 = bf16[2048,4,2304]{0,2,1:T(8,128)(2,1)} fusion(bf16[2048,4,2304]{0,2,1:T(8,128)(2,1)} %get-tuple-element.205, s32[]{:T(128)S(6)} %select_n.54, bf16[128,2048]{1,0:T(8,128)(2,1)} %get-tuple-element.217, bf16[4,128,2304]{2,1,0:T(8,128)(2,1)S(1)} %get-tuple-element.216), kind=kOutput, calls=%fused_computation.8.clone.1 | convolution fusion | flops 1212678144 | bytes 10552320 | tf_op jit(solution)/shard_map/while/body/dot_general | solution.py:20
  281.3 6.9 %fusion.43 = f32[128,2048]{1,0:T(8,128)S(1)} fusion(f32[128,2048]{1,0:T(8,128)S(1)} %get-tuple-element.206, bf16[2048,4,2304]{2,0,1:T(8,128)(2,1)} %get-tuple-element.218, s32[]{:T(128)S(6)} %select_n.54, bf16[4,128,2304]{2,1,0:T(8,128)(2,1)S(1)} %get-tuple-element.216), kind=kOutput, calls=%fused_computation.12.clone.1 | convolution fusion | flops 1208221696 | bytes 12125184 | tf_op jit(solution)/shard_map/while/body/dot_general | solution.py:26
  288.2 9.0 %fusion.22 = f32[128,64]{1,0:T(8,128)S(1)} fusion(f32[128,2048]{1,0:T(8,128)S(1)} %get-tuple-element.60, s32[2048]{0:T(1024)S(1)} %iota_add_fusion, s32[128,64]{1,0:T(8,128)S(1)} %copy.17), kind=kLoop, calls=%fused_computation.22 | loop fusion | flops 50323456 | bytes 1122304 | tf_op jit(solution)/shard_map/reduce_sum | solution.py:72
  297.2 0.1 copy.22
  297.4 0.0 copy-start.3
  297.4 0.6 copy-done.3
  298.0 0.0 all-reduce.5.cloned.1.call-update
  298.0 0.5 broadcast_multiply_fusion
  298.6 0.0 copy-start.1
  298.6 57.6 %copy.23 = bf16[2048,4,2304]{2,1,0:T(4,128)(2,1)} copy(bf16[2048,4,2304]{0,2,1:T(8,128)(2,1)} %get-tuple-element.88) | data formatting | bytes 75497472
  356.2 63.9 %all-reduce.5.cloned.1.call-done = f32[4,128,64]{1,2,0:T(8,128)} async-done(((f32[4,128,64]{1,2,0:T(8,128)}), f32[4,128,64]{1,2,0:T(8,128)}) %all-reduce.5.cloned.1.call-update) | async-done | bytes 131088 | tf_op jit(solution)/shard_map/psum | solution.py:76
  420.1 1.6 copy.51
  421.6 0.0 copy-done.1
  (4 shorter events, 0.1 us)
Async XLA Ops:
  7.2 26.8 %copy-start = (s32[4,128,64]{1,2,0:T(8,128)S(1)}, s32[4,128,64]{1,2,0:T(8,128)}, u32[]{:S(2)}) copy-start(s32[4,128,64]{1,2,0:T(8,128)} %param.10) | copy-start | bytes 393220
  7.2 212.0 %all-reduce.3.cloned.1.call-start = ((), (), s32[]{:S(2)}) async-start(), calls=%async_computation | async-start | bytes 9437184 | tf_op jit(solution)/shard_map/psum | solution.py:54
  46.5 172.7 %copy-start.4 = (f32[4,2304]{1,0:T(4,128)S(1)}, f32[4,2304]{1,0:T(4,128)}, u32[]{:S(2)}) copy-start(f32[4,2304]{1,0:T(4,128)} %param.12) | copy-start | bytes 110596
  73.4 149.9 %copy-start.2 = (bf16[128,2048]{1,0:T(8,128)(2,1)}, bf16[128,2048]{1,0:T(8,128)(2,1)S(1)}, u32[]{:S(2)}) copy-start(bf16[128,2048]{1,0:T(8,128)(2,1)S(1)} %get-tuple-element.230) | copy-start | bytes 1572868
  73.4 346.6 %all-reduce.5.cloned.1.call-start = ((), (), s32[]{:S(2)}) async-start(), calls=%async_computation.1 | async-start | bytes 262144 | tf_op jit(solution)/shard_map/psum | solution.py:76
  297.4 0.7 copy-start.3
  298.6 123.1 %copy-start.1 = (s32[4,128,64]{1,2,0:T(8,128)S(1)}, s32[4,128,64]{1,2,0:T(8,128)}, u32[]{:S(2)}) copy-start(s32[4,128,64]{1,2,0:T(8,128)} %param.10) | copy-start | bytes 393220
Sparse Core Ops, SparseCore 0:
  73.5 145.6 all-reduce.2
  298.2 121.8 all-reduce.4
where the time goes:
time: 430 us; the launch traced here: 428 us
  waiting for transfers between devices  210 us (49%)
  local copies, waits for them, and re-layouts  107 us (25%)
  matrix products  73 us (17%)
  other arithmetic  24.2 us (6%)
  between operations  14.2 us (3%)
    psum x1, waiting for transfers between devices, on_device(): recon_sum = lax.psum(partials, ('layer', 'latent'))  146 us
    psum x1, waiting for transfers between devices, on_device(): code_grad = lax.psum(code_parts, ('layer', 'latent'))  63.9 us
    unnamed x12, local copies, waits for them, and re-layouts  59.9 us
    dot_general x4, matrix products, contract_cols(): lax.dot_general(left, right, (((1,), (1,)), ((), ())), preferred_element_...  27.6 us
    while x1, local copies, waits for them, and re-layouts, on_device(): partials = lax.fori_loop(source, stop_at, forward_step, partials)  25.9 us
    dot_general x4, matrix products, contract_rows(): lax.dot_general(left, right, (((0,), (0,)), ((), ())), preferred_element_...  24.6 us
    dot_general x4, matrix products, forward_step(): jnp.dot(dense_codes, weight_slab, preferred_element_type=jnp.float32)  20.9 us
    broadcast_in_dim x1, local copies, waits for them, and re-layouts, on_device(): jnp.zeros(decoder.shape, jnp.bfloat16)  12.5 us
  transfers between devices with their start and end apart: 2, of which 2 were waited for; matrix products, arithmetic and copies ran while one was open for 14% of the time, Pallas kernels for 0%

commit v1 on v0

--- a/solution.py
+++ b/solution.py
@@ -51,7 +51,7 @@
     partials = jnp.zeros((LAYERS, TOKENS, D), jnp.float32)
     stop_at = LAYERS
     partials = lax.fori_loop(source, stop_at, forward_step, partials)
-    recon_sum = lax.psum(partials, ("layer", "latent"))
+    recon_sum = lax.psum(lax.psum(partials, "latent"), "layer")
     residual = recon_sum + bias[:, None, :] - target.astype(jnp.float32)
     layer_error = jnp.mean(residual * residual, axis=(1, 2))
     error_b = residual.astype(jnp.bfloat16)

time: 430 us -> 548 us (1.27)
  waiting for transfers between devices: 210 us -> 327 us
    psum x1 -> x2, waiting for transfers between devices: 146 us -> 262 us  [on_device(): recon_sum = lax.psum(lax.psum(partials, 'latent'), 'layer')]
  transfers between devices with their start and end apart: 2 -> 3, of which waited for: 2 -> 3; matrix products, arithmetic and copies ran while one was open for 14% -> 11% of each run, Pallas kernels for 0% -> 0%
where the time goes in v1:
time: 548 us; the launch traced here: 546 us
  waiting for transfers between devices  327 us (60%)
  local copies, waits for them, and re-layouts  107 us (20%)
  matrix products  73 us (13%)
  other arithmetic  24.2 us (4%)
  between operations  13.9 us (3%)
    psum x2, waiting for transfers between devices, on_device(): recon_sum = lax.psum(lax.psum(partials, 'latent'), 'layer')  262 us
    psum x1, waiting for transfers between devices, on_device(): code_grad = lax.psum(code_parts, ('layer', 'latent'))  65.5 us
    unnamed x12, local copies, waits for them, and re-layouts  59.9 us
    dot_general x4, matrix products, contract_cols(): lax.dot_general(left, right, (((1,), (1,)), ((), ())), preferred_element_...  27.6 us
    while x1, local copies, waits for them, and re-layouts, on_device(): partials = lax.fori_loop(source, stop_at, forward_step, partials)  25.9 us
    dot_general x4, matrix products, contract_rows(): lax.dot_general(left, right, (((0,), (0,)), ((), ())), preferred_element_...  24.6 us
    dot_general x4, matrix products, forward_step(): jnp.dot(dense_codes, weight_slab, preferred_element_type=jnp.float32)  20.9 us
    broadcast_in_dim x1, local copies, waits for them, and re-layouts, on_device(): jnp.zeros(decoder.shape, jnp.bfloat16)  12.5 us
  transfers between devices with their start and end apart: 3, of which 3 were waited for; matrix products, arithmetic and copies ran while one was open for 11% of the time, Pallas kernels for 0%

profile of v1, /device:TPU:0, one launch (start us, length us, event | category | flops | bytes accessed | tf_op | source)
XLA Modules:
  0.0 545.9 jit_solution(17231205610036496668)
XLA Ops:
  7.2 0.0 copy-start
  7.2 0.0 all-reduce.4.cloned.1.call-start
  7.2 25.9 %copy.19 = bf16[2048,4,2304]{2,0,1:T(8,128)(2,1)} copy(bf16[2048,4,2304]{2,1,0:T(4,128)(2,1)} %param.9) | data formatting | bytes 75497472 | tf_op jit(solution)/shard_map/while | solution.py:53
  33.1 0.7 bitcast_convert_fusion
  33.8 0.1 copy.18
  34.0 0.0 copy-done
  34.0 0.1 copy.17
  34.1 9.8 %fusion.21 = bf16[128,2048]{1,0:T(8,128)(2,1)S(1)} fusion(f32[128,64]{1,0:T(8,128)S(1)} %copy.18, s32[2048]{0:T(1024)S(1)} %iota_add_fusion, s32[128,64]{1,0:T(8,128)S(1)} %copy.17), kind=kLoop, calls=%fused_computation.21 | loop fusion | flops 50069504 | bytes 598016 | tf_op jit(solution)/shard_map/reduce_sum | solution.py:15
  43.9 2.6 broadcast_in_dim.51.clone
  46.5 26.9 %while.22 = (s32[]{:T(128)}, f32[4,128,2304]{2,1,0:T(8,128)}, bf16[2048,4,2304]{2,0,1:T(8,128)(2,1)}, bf16[128,2048]{1,0:T(8,128)(2,1)S(1)}, s32[]{:T(128)}, /*index=5*/s32[]{:T(128)}, s32[]{:T(128)}) while((s32[]{:T(128)}, f32[4,128,2304]{2,1,0:T(8,128)}, bf16[2048,4,2304]{2,0,1:T(8,128)(2,1)}, bf16[128,2048]{1,0:T(8,128)(2,1)S(1)}, ...), condition=%wide.region_2.3_spmd, body=%wide.region_1.2_spmd.sunk | while | flops 1207959552 | bytes 15859839 | solution.py:53
  46.5 5.2 fusion.37
  51.7 0.4 copy.30
  52.1 1.1 constant_dynamic-update-slice_fusion.3
  53.2 5.2 fusion.37
  58.4 0.4 copy.30
  58.8 1.1 constant_dynamic-update-slice_fusion.3
  59.9 5.2 fusion.37
  65.1 0.4 copy.30
  65.5 1.1 constant_dynamic-update-slice_fusion.3
  66.6 5.2 fusion.37
  71.8 0.4 copy.30
  72.2 1.2 constant_dynamic-update-slice_fusion.3
  73.4 0.0 copy-start.2
  73.4 0.0 copy-start.4
  73.4 0.0 all-reduce.4.cloned.1.call-update
  73.4 0.0 all-reduce.6.cloned.1.call-start
  73.5 172.9 %all-reduce.4.cloned.1.call-done = f32[4,128,2304]{2,1,0:T(8,128)} async-done(((f32[4,128,2304]{2,1,0:T(8,128)}), f32[4,128,2304]{2,1,0:T(8,128)}) %all-reduce.4.cloned.1.call-update) | async-done | bytes 4718608 | tf_op jit(solution)/shard_map/psum | solution.py:54
  246.4 0.0 all-reduce.6.cloned.1.call-update
  246.4 0.0 all-reduce.8.cloned.1.call-start
  246.4 88.8 %all-reduce.6.cloned.1.call-done = f32[4,128,2304]{2,1,0:T(8,128)} async-done(((f32[4,128,2304]{2,1,0:T(8,128)}), f32[4,128,2304]{2,1,0:T(8,128)}) %all-reduce.6.cloned.1.call-update) | async-done | bytes 4718608 | tf_op jit(solution)/shard_map/psum | solution.py:54
  335.3 0.0 copy-done.4
  335.3 4.1 fusion.23
  339.4 0.0 copy-done.2
  339.4 12.5 %broadcast_in_dim.54 = bf16[2048,4,2304]{0,2,1:T(8,128)(2,1)} broadcast(bf16[]{:T(256)} %constant.88.clone.1), dimensions={} | broadcast | bytes 37748736 | tf_op jit(solution)/shard_map/broadcast_in_dim | solution.py:68
  351.9 0.1 broadcast_in_dim.55
  352.0 52.3 %while.23 = (s32[]{:T(128)}, bf16[2048,4,2304]{0,2,1:T(8,128)(2,1)}, f32[128,2048]{1,0:T(8,128)S(1)}, bf16[4,128,2304]{2,1,0:T(8,128)(2,1)S(1)}, bf16[128,2048]{...) while((s32[]{:T(128)}, bf16[2048,4,2304]{0,2,1:T(8,128)(2,1)}, ...), condition=%wide.region_7.8_spmd, body=%wide.region_6.7_spmd.sunk | while | flops 2420899840 | bytes 22677640 | solution.py:71
  352.0 6.1 %fusion.42 = bf16[2048,4,2304]{0,2,1:T(8,128)(2,1)} fusion(bf16[2048,4,2304]{0,2,1:T(8,128)(2,1)} %get-tuple-element.205, s32[]{:T(128)S(6)} %select_n.54, bf16[128,2048]{1,0:T(8,128)(2,1)} %get-tuple-element.217, bf16[4,128,2304]{2,1,0:T(8,128)(2,1)S(1)} %get-tuple-element.216), kind=kOutput, calls=%fused_computation.8.clone.1 | convolution fusion | flops 1212678144 | bytes 10552320 | tf_op jit(solution)/shard_map/while/body/dot_general | solution.py:20
  358.2 6.9 %fusion.43 = f32[128,2048]{1,0:T(8,128)S(1)} fusion(f32[128,2048]{1,0:T(8,128)S(1)} %get-tuple-element.206, bf16[2048,4,2304]{2,0,1:T(8,128)(2,1)} %get-tuple-element.218, s32[]{:T(128)S(6)} %select_n.54, bf16[4,128,2304]{2,1,0:T(8,128)(2,1)S(1)} %get-tuple-element.216), kind=kOutput, calls=%fused_computation.12.clone.1 | convolution fusion | flops 1208221696 | bytes 12125184 | tf_op jit(solution)/shard_map/while/body/dot_general | solution.py:26
  365.1 6.1 %fusion.42 = bf16[2048,4,2304]{0,2,1:T(8,128)(2,1)} fusion(bf16[2048,4,2304]{0,2,1:T(8,128)(2,1)} %get-tuple-element.205, s32[]{:T(128)S(6)} %select_n.54, bf16[128,2048]{1,0:T(8,128)(2,1)} %get-tuple-element.217, bf16[4,128,2304]{2,1,0:T(8,128)(2,1)S(1)} %get-tuple-element.216), kind=kOutput, calls=%fused_computation.8.clone.1 | convolution fusion | flops 1212678144 | bytes 10552320 | tf_op jit(solution)/shard_map/while/body/dot_general | solution.py:20
  371.2 6.9 %fusion.43 = f32[128,2048]{1,0:T(8,128)S(1)} fusion(f32[128,2048]{1,0:T(8,128)S(1)} %get-tuple-element.206, bf16[2048,4,2304]{2,0,1:T(8,128)(2,1)} %get-tuple-element.218, s32[]{:T(128)S(6)} %select_n.54, bf16[4,128,2304]{2,1,0:T(8,128)(2,1)S(1)} %get-tuple-element.216), kind=kOutput, calls=%fused_computation.12.clone.1 | convolution fusion | flops 1208221696 | bytes 12125184 | tf_op jit(solution)/shard_map/while/body/dot_general | solution.py:26
  378.1 6.2 %fusion.42 = bf16[2048,4,2304]{0,2,1:T(8,128)(2,1)} fusion(bf16[2048,4,2304]{0,2,1:T(8,128)(2,1)} %get-tuple-element.205, s32[]{:T(128)S(6)} %select_n.54, bf16[128,2048]{1,0:T(8,128)(2,1)} %get-tuple-element.217, bf16[4,128,2304]{2,1,0:T(8,128)(2,1)S(1)} %get-tuple-element.216), kind=kOutput, calls=%fused_computation.8.clone.1 | convolution fusion | flops 1212678144 | bytes 10552320 | tf_op jit(solution)/shard_map/while/body/dot_general | solution.py:20
  384.3 6.9 %fusion.43 = f32[128,2048]{1,0:T(8,128)S(1)} fusion(f32[128,2048]{1,0:T(8,128)S(1)} %get-tuple-element.206, bf16[2048,4,2304]{2,0,1:T(8,128)(2,1)} %get-tuple-element.218, s32[]{:T(128)S(6)} %select_n.54, bf16[4,128,2304]{2,1,0:T(8,128)(2,1)S(1)} %get-tuple-element.216), kind=kOutput, calls=%fused_computation.12.clone.1 | convolution fusion | flops 1208221696 | bytes 12125184 | tf_op jit(solution)/shard_map/while/body/dot_general | solution.py:26
  391.2 6.1 %fusion.42 = bf16[2048,4,2304]{0,2,1:T(8,128)(2,1)} fusion(bf16[2048,4,2304]{0,2,1:T(8,128)(2,1)} %get-tuple-element.205, s32[]{:T(128)S(6)} %select_n.54, bf16[128,2048]{1,0:T(8,128)(2,1)} %get-tuple-element.217, bf16[4,128,2304]{2,1,0:T(8,128)(2,1)S(1)} %get-tuple-element.216), kind=kOutput, calls=%fused_computation.8.clone.1 | convolution fusion | flops 1212678144 | bytes 10552320 | tf_op jit(solution)/shard_map/while/body/dot_general | solution.py:20
  397.4 6.9 %fusion.43 = f32[128,2048]{1,0:T(8,128)S(1)} fusion(f32[128,2048]{1,0:T(8,128)S(1)} %get-tuple-element.206, bf16[2048,4,2304]{2,0,1:T(8,128)(2,1)} %get-tuple-element.218, s32[]{:T(128)S(6)} %select_n.54, bf16[4,128,2304]{2,1,0:T(8,128)(2,1)S(1)} %get-tuple-element.216), kind=kOutput, calls=%fused_computation.12.clone.1 | convolution fusion | flops 1208221696 | bytes 12125184 | tf_op jit(solution)/shard_map/while/body/dot_general | solution.py:26
  404.3 9.0 %fusion.22 = f32[128,64]{1,0:T(8,128)S(1)} fusion(f32[128,2048]{1,0:T(8,128)S(1)} %get-tuple-element.60, s32[2048]{0:T(1024)S(1)} %iota_add_fusion, s32[128,64]{1,0:T(8,128)S(1)} %copy.17), kind=kLoop, calls=%fused_computation.22 | loop fusion | flops 50323456 | bytes 1122304 | tf_op jit(solution)/shard_map/reduce_sum | solution.py:72
  413.3 0.1 copy.22
  413.4 0.0 copy-start.3
  413.4 0.6 copy-done.3
  414.1 0.0 all-reduce.8.cloned.1.call-update
  414.1 0.5 broadcast_multiply_fusion
  414.6 0.0 copy-start.1
  414.6 57.6 %copy.23 = bf16[2048,4,2304]{2,1,0:T(4,128)(2,1)} copy(bf16[2048,4,2304]{0,2,1:T(8,128)(2,1)} %get-tuple-element.88) | data formatting | bytes 75497472
  472.2 65.5 %all-reduce.8.cloned.1.call-done = f32[4,128,64]{1,2,0:T(8,128)} async-done(((f32[4,128,64]{1,2,0:T(8,128)}), f32[4,128,64]{1,2,0:T(8,128)}) %all-reduce.8.cloned.1.call-update) | async-done | bytes 131088 | tf_op jit(solution)/shard_map/psum | solution.py:76
  537.8 1.6 copy.52
  539.3 0.0 copy-done.1
  (4 shorter events, 0.1 us)
Async XLA Ops:
  7.2 26.8 %copy-start = (s32[4,128,64]{1,2,0:T(8,128)S(1)}, s32[4,128,64]{1,2,0:T(8,128)}, u32[]{:S(2)}) copy-start(s32[4,128,64]{1,2,0:T(8,128)} %param.10) | copy-start | bytes 393220
  7.2 239.2 %all-reduce.4.cloned.1.call-start = ((), (), s32[]{:S(2)}) async-start(), calls=%async_computation | async-start | bytes 9437184 | tf_op jit(solution)/shard_map/psum | solution.py:54
  73.4 266.0 %copy-start.2 = (bf16[128,2048]{1,0:T(8,128)(2,1)}, bf16[128,2048]{1,0:T(8,128)(2,1)S(1)}, u32[]{:S(2)}) copy-start(bf16[128,2048]{1,0:T(8,128)(2,1)S(1)} %get-tuple-element.231) | copy-start | bytes 1572868
  73.4 261.9 %copy-start.4 = (f32[4,2304]{1,0:T(4,128)S(1)}, f32[4,2304]{1,0:T(4,128)}, u32[]{:S(2)}) copy-start(f32[4,2304]{1,0:T(4,128)} %param.12) | copy-start | bytes 110596
  73.4 261.8 %all-reduce.6.cloned.1.call-start = ((), (), s32[]{:S(2)}) async-start(), calls=%async_computation.1 | async-start | bytes 9437184 | tf_op jit(solution)/shard_map/psum | solution.py:54
  246.4 291.4 %all-reduce.8.cloned.1.call-start = ((), (), s32[]{:S(2)}) async-start(), calls=%async_computation.2 | async-start | bytes 262144 | tf_op jit(solution)/shard_map/psum | solution.py:76
  413.4 0.7 copy-start.3
  414.6 124.7 %copy-start.1 = (s32[4,128,64]{1,2,0:T(8,128)S(1)}, s32[4,128,64]{1,2,0:T(8,128)}, u32[]{:S(2)}) copy-start(s32[4,128,64]{1,2,0:T(8,128)} %param.10) | copy-start | bytes 393220
Sparse Core Ops, SparseCore 0:
  73.5 172.7 all-reduce.3
  249.7 85.5 all-reduce.5
  414.2 123.4 all-reduce.7
